TPU v7x, 32 devices: a whole 2x2x4 slice. The times are simulated.
32 devices in a mesh: section: 4 (over x, core), obs: 8 (over z, y).
Axes of the slice: x: 2, y: 2, z: 4, core: 2. Of those that a mesh axis runs over, the one named last changes fastest.
Arguments:
- predictors: bfloat16 [4, 4, 20, 32768], P('section', None, None, 'obs'), may hold values from -5 to 5
- departures: float32 [4, 4, 32768], P('section', None, 'obs'), may hold values from -30 to 30
- obs_precision: float32 [4, 4, 32768], P('section', None, 'obs'), may hold values from 0.3 to 3
- qc_pass: int32 [4, 4, 32768], P('section', None, 'obs'), may hold values 0 or 1
- block_channel: int32 [4, 4, 256], P('section', None, 'obs'), may hold values from 0 to 2047, as said below
- stream_order: int32 [4], replicated, may hold values from 0 to 3, each once
- prior_coeffs: float32 [4, 20, 2048], P(None, None, 'obs'), may hold values from -1 to 1
- prior_info: float32 [4, 210, 2048], P(None, None, 'obs'), may hold values from -1 to 32, as said below
- memory_factor: float32 [2048], P('obs'), may hold values from 0.5 to 0.98
Outputs:
- coeffs: float32 [4, 4, 20, 2048], P('section', None, None, 'obs')
- information: float32 [4, 4, 210, 2048], P('section', None, None, 'obs')
Inputs may be any that keep to these rules, and one draw needn't show every extreme that they name: `block_channel`: among the 32 row blocks of one index of obs, at most 8 have channels in any one range of the 256 channels from a multiple of 256; in every window and stream one such range holds exactly 8 blocks of every index of obs. `stream_order`: each stream appears once. `prior_info`: for every stream and channel the 210 entries are the upper triangle, row by row, of a symmetric positive definite matrix of order 20.
All inputs are finite; a program needn't handle non-finite values. No bound on the sum of `qc_pass` on one device may be relied on, other than what follows from the above.
Results may differ from a plain program's by a relative error of at most 0.0038.
Values sent between devices are 32-bit elements; how exact they have to be, the bound alone decides.
No kernel may reach another device: no remote copies, remote signals or barrier semaphores. Data moves between devices by JAX's collectives and lax.ppermute only.
A program may use at most 64 MiB of HBM per device.

v0:
```python
import jax
import jax.numpy as jnp
import numpy as np
from jax import lax
from jax.sharding import PartitionSpec as P

HUBER_SQ = 9.0
PRIOR_WEIGHT = 64.0


def from_behind(array, axis, by):
    size = lax.axis_size(axis)
    pairs = [(i, i + by) for i in range(size) if 0 <= i + by < size]
    return lax.ppermute(array, axis, pairs)


def upper_positions(dimension):
    return np.array(
        [i * dimension + j for i in range(dimension) for j in range(i, dimension)], dtype=np.int32
    )


def solve_packed(packed, target):
    dimension = target.shape[0]
    placing = {}
    counter = 0
    for i in range(dimension):
        for j in range(i, dimension):
            placing[i, j] = counter
            counter += 1
    factor = [[None] * dimension for i in range(dimension)]
    for j in range(dimension):
        pivot_root = jnp.sqrt(
            packed[placing[j, j]] - sum((factor[j][k] * factor[j][k] for k in range(j)))
        )
        factor[j][j] = pivot_root
        for i in range(j + 1, dimension):
            factor[i][j] = (
                packed[placing[j, i]] - sum((factor[i][k] * factor[j][k] for k in range(j)))
            ) / pivot_root
    forward = []
    for i in range(dimension):
        forward.append(
            (target[i] - sum((factor[i][k] * forward[k] for k in range(i)))) / factor[i][i]
        )
    backward = [None] * dimension
    for i in reversed(range(dimension)):
        backward[i] = (
            forward[i] - sum((factor[k][i] * backward[k] for k in range(i + 1, dimension)))
        ) / factor[i][i]
    return jnp.stack(backward)


def block_terms(predicted, departed, precision, passed, block_coeffs):
    pred_count, row_count = predicted.shape
    block_count = block_coeffs.shape[1]
    block_width = row_count // block_count
    upper_index = upper_positions(pred_count)
    shaped = predicted.reshape(pred_count, block_count, block_width)
    offset = jnp.sum(shaped.astype(jnp.float32) * block_coeffs[:, :, None], axis=0)
    residual = departed.reshape(block_count, block_width) - offset
    scale_row = precision.reshape(block_count, block_width)
    weight = (
        passed.reshape(block_count, block_width).astype(jnp.float32)
        * scale_row
        / (1.0 + scale_row * residual * residual / HUBER_SQ)
    )
    weighted = (weight[None] * shaped.astype(jnp.float32)).astype(jnp.bfloat16)
    chi_square = jnp.sum(weight * residual * residual)
    passed_count = jnp.sum(passed.astype(jnp.float32))
    gram_full = lax.dot_general(
        weighted, shaped, (((2,), (2,)), ((1,), (1,))), preferred_element_type=jnp.float32
    )
    gram_upper = gram_full.reshape(block_count, pred_count * pred_count)[:, upper_index]
    gradient = jnp.sum(weighted.astype(jnp.float32) * residual[None], axis=2).T
    return (jnp.concatenate([gram_upper, gradient], axis=1), jnp.stack([chi_square, passed_count]))


def local(
    predictors,
    departures,
    obs_precision,
    qc_pass,
    block_channel,
    stream_order,
    prior_coeffs,
    prior_info,
    memory_factor,
):
    section_count = lax.axis_size("section")
    obs_devices = lax.axis_size("obs")
    section_place = lax.axis_index("section")
    stream_count = stream_order.shape[0]
    local_channels = memory_factor.shape[0]
    block_count = block_channel.shape[2]
    pred_count = prior_coeffs.shape[1]
    tri_count = prior_info.shape[1]
    column_count = tri_count + pred_count
    capacity = 2 * block_count // obs_devices
    local_line = jnp.arange(local_channels, dtype=jnp.float32)
    owner_line = jnp.arange(obs_devices, dtype=jnp.int32)
    slot_line = jnp.arange(obs_devices * capacity, dtype=jnp.int32)
    highest = lax.Precision.HIGHEST

    def pack_blocks(block_sums, channel):
        owner_index = channel // local_channels
        inner_channel = channel % local_channels
        owner_hot = (owner_index[:, None] == owner_line[None, :]).astype(jnp.int32)
        ranking = jnp.sum((jnp.cumsum(owner_hot, axis=0) - 1) * owner_hot, axis=1)
        slot_of = owner_index * capacity + ranking
        placing = (slot_of[:, None] == slot_line[None, :]).astype(jnp.float32)
        send_rows = lax.dot_general(
            placing,
            block_sums,
            (((0,), (0,)), ((), ())),
            precision=highest,
            preferred_element_type=jnp.float32,
        ).reshape(obs_devices, capacity, column_count)
        send_channel = (
            lax.dot_general(
                placing,
                (inner_channel + 1).astype(jnp.float32),
                (((0,), (0,)), ((), ())),
                precision=highest,
                preferred_element_type=jnp.float32,
            ).reshape(obs_devices, capacity)
            - 1.0
        )
        return (send_rows, send_channel)

    def unpack_blocks(got_rows, got_channel):
        gather_hot = (got_channel.reshape(-1)[:, None] == local_line[None, :]).astype(jnp.float32)
        return lax.dot_general(
            got_rows.reshape(-1, column_count),
            gather_hot,
            (((0,), (0,)), ((), ())),
            precision=highest,
            preferred_element_type=jnp.float32,
        )

    def window_work(state_now, streams):
        beta_prior = state_now[:, :pred_count]
        info_prior = state_now[:, pred_count:]
        all_coeffs = lax.all_gather(beta_prior, "obs", axis=2, tiled=True)
        channel = jnp.take(block_channel[0], streams, axis=0)
        block_coeffs = jax.vmap(lambda coeff_rows, chan: jnp.take(coeff_rows, chan, axis=1))(
            all_coeffs, channel
        )
        block_sums, statistics = jax.vmap(block_terms)(
            jnp.take(predictors[0], streams, axis=0),
            jnp.take(departures[0], streams, axis=0),
            jnp.take(obs_precision[0], streams, axis=0),
            jnp.take(qc_pass[0], streams, axis=0),
            block_coeffs,
        )
        totals = lax.psum(statistics, "obs")
        send_rows, send_channel = jax.vmap(pack_blocks)(block_sums, channel)
        got_rows, got_channel = (
            lax.all_to_all(send_rows, "obs", split_axis=1, concat_axis=1, tiled=True),
            lax.all_to_all(send_channel, "obs", split_axis=1, concat_axis=1, tiled=True),
        )
        normal = jax.vmap(unpack_blocks)(got_rows, got_channel)
        inflation = (totals[:, 0] + PRIOR_WEIGHT) / (totals[:, 1] + PRIOR_WEIGHT)
        info_post = info_prior + normal[:, :tri_count] / inflation[:, None, None]
        beta_post = beta_prior + jax.vmap(solve_packed)(
            info_post, normal[:, tri_count:] / inflation[:, None, None]
        )
        outgoing = jnp.concatenate([beta_post, memory_factor[None, None, :] * info_post], axis=1)
        incoming = from_behind(outgoing, "section", 1)
        return (beta_post, info_post, incoming)

    def fresh_of(streams):
        return jnp.concatenate(
            [jnp.take(prior_coeffs, streams, axis=0), jnp.take(prior_info, streams, axis=0)], axis=1
        )

    coeff_start = jnp.zeros((1, stream_count, pred_count, local_channels), jnp.float32)
    info_start = jnp.zeros((1, stream_count, tri_count, local_channels), jnp.float32)

    def tick_step(t, loop_state):
        incoming, coeff_out, info_out = loop_state
        entry_index = t - section_place
        usable = (entry_index >= 0) & (entry_index < stream_count)
        slot_index = jnp.clip(entry_index, 0, stream_count - 1)
        streams = lax.dynamic_slice_in_dim(stream_order, slot_index, 1, 0)
        state_now = jnp.where(
            (section_place == 0) | jnp.logical_not(usable), fresh_of(streams), incoming
        )
        beta_post, info_post, incoming = window_work(state_now, streams)

        def store_entry(buffer, result):
            current = lax.dynamic_slice_in_dim(buffer, slot_index, 1, 1)
            updated = jnp.where(usable, result[None], current)
            return lax.dynamic_update_slice_in_dim(buffer, updated, slot_index, 1)

        return (incoming, store_entry(coeff_out, beta_post), store_entry(info_out, info_post))

    initial = (jnp.zeros((1, column_count, local_channels), jnp.float32), coeff_start, info_start)
    final_state = lax.fori_loop(0, stream_count + section_count - 1, tick_step, initial)
    return (final_state[1], final_state[2])


def solution(mesh):
    in_specs = (
        P("section", None, None, "obs"),
        P("section", None, "obs"),
        P("section", None, "obs"),
        P("section", None, "obs"),
        P("section", None, "obs"),
        P(),
        P(None, None, "obs"),
        P(None, None, "obs"),
        P("obs"),
    )
    out_specs = (P("section", None, None, "obs"), P("section", None, None, "obs"))
    return jax.shard_map(local, mesh=mesh, in_specs=in_specs, out_specs=out_specs, check_vma=False)
```

profile of v0, /device:TPU:0, one launch (start us, length us, event | category | flops | bytes accessed | tf_op | source)
XLA Modules:
  0.0 683.1 jit_solution(5905409147109336993)
XLA Ops:
  2.9 679.2 %while.38 = (s32[]{:T(128)}, f32[1,230,256]{2,1,0:T(8,128)S(1)}, f32[1,4,20,256]{3,1,2,0:T(4,128)S(1)}, f32[1,4,210,256]{3,1,2,0:T(4,128)S(1)}, s32[]{:T(128)}, ...) while((s32[]{:T(128)}, f32[1,230,256]{2,1,0:T(8,128)S(1)}, ...), condition=%wide.region_8.10_spmd.clone.clone, body=%wide.region_0.9_spmd.sunk.clone.clone.sunk | while | flops 57759508 | bytes 13853709 | solution.py:199
  7.5 7.3 %all-to-all-start.1 = ((f32[1,8,8]{2,0,1:T(1,128)}), f32[1,8,8]{2,0,1:T(1,128)S(1)}, u32[]{:S(2)}, u32[]{:S(2)}) async-start(f32[1,8,8]{2,0,1:T(1,128)} %bitcast.2454), calls=%async_computation.1 | async-start | bytes 8192 | tf_op jit(solution)/shard_map/while/body/eval_jaxpr/all_to_all | solution.py:160
  17.2 31.2 %all_gather.15 = f32[1,20,2048]{2,1,0:T(8,128)S(1)} all-gather(f32[1,20,256]{2,1,0:T(8,128)S(1)} %slice.5342), channel_id=1, replica_groups=mesh['section'=4,'obs'=8] {'obs'}, dimensions={2}, use_global_device_ids=true | all-gather | bytes 184320 | tf_op jit(solution)/shard_map/while/body/eval_jaxpr/all_gather | solution.py:144
  55.2 21.5 %psum.19 = f32[1,2]{1,0:T(1,128)S(1)} all-reduce(f32[1,2]{1,0:T(1,128)S(1)} %maximum_bitcast_fusion.6), channel_id=1, replica_groups=mesh['section'=4,'obs'=8] {'obs'}, use_global_device_ids=true, to_apply=%region_7.8 | all-reduce | flops 2 | bytes 16 | tf_op jit(solution)/shard_map/while/body/eval_jaxpr/psum | solution.py:156
  84.2 5.6 all-to-all-done
  97.6 5.9 dynamic_update_slice.31
  113.9 31.1 %all_gather.15 = f32[1,20,2048]{2,1,0:T(8,128)S(1)} all-gather(f32[1,20,256]{2,1,0:T(8,128)S(1)} %slice.5342), channel_id=1, replica_groups=mesh['section'=4,'obs'=8] {'obs'}, dimensions={2}, use_global_device_ids=true | all-gather | bytes 184320 | tf_op jit(solution)/shard_map/while/body/eval_jaxpr/all_gather | solution.py:144
  151.7 21.3 %psum.19 = f32[1,2]{1,0:T(1,128)S(1)} all-reduce(f32[1,2]{1,0:T(1,128)S(1)} %maximum_bitcast_fusion.6), channel_id=1, replica_groups=mesh['section'=4,'obs'=8] {'obs'}, use_global_device_ids=true, to_apply=%region_7.8 | all-reduce | flops 2 | bytes 16 | tf_op jit(solution)/shard_map/while/body/eval_jaxpr/psum | solution.py:156
  194.0 5.9 dynamic_update_slice.31
  210.3 31.1 %all_gather.15 = f32[1,20,2048]{2,1,0:T(8,128)S(1)} all-gather(f32[1,20,256]{2,1,0:T(8,128)S(1)} %slice.5342), channel_id=1, replica_groups=mesh['section'=4,'obs'=8] {'obs'}, dimensions={2}, use_global_device_ids=true | all-gather | bytes 184320 | tf_op jit(solution)/shard_map/while/body/eval_jaxpr/all_gather | solution.py:144
  248.1 21.3 %psum.19 = f32[1,2]{1,0:T(1,128)S(1)} all-reduce(f32[1,2]{1,0:T(1,128)S(1)} %maximum_bitcast_fusion.6), channel_id=1, replica_groups=mesh['section'=4,'obs'=8] {'obs'}, use_global_device_ids=true, to_apply=%region_7.8 | all-reduce | flops 2 | bytes 16 | tf_op jit(solution)/shard_map/while/body/eval_jaxpr/psum | solution.py:156
  290.3 5.9 dynamic_update_slice.31
  306.6 31.1 %all_gather.15 = f32[1,20,2048]{2,1,0:T(8,128)S(1)} all-gather(f32[1,20,256]{2,1,0:T(8,128)S(1)} %slice.5342), channel_id=1, replica_groups=mesh['section'=4,'obs'=8] {'obs'}, dimensions={2}, use_global_device_ids=true | all-gather | bytes 184320 | tf_op jit(solution)/shard_map/while/body/eval_jaxpr/all_gather | solution.py:144
  344.4 21.5 %psum.19 = f32[1,2]{1,0:T(1,128)S(1)} all-reduce(f32[1,2]{1,0:T(1,128)S(1)} %maximum_bitcast_fusion.6), channel_id=1, replica_groups=mesh['section'=4,'obs'=8] {'obs'}, use_global_device_ids=true, to_apply=%region_7.8 | all-reduce | flops 2 | bytes 16 | tf_op jit(solution)/shard_map/while/body/eval_jaxpr/psum | solution.py:156
  386.9 5.9 dynamic_update_slice.31
  403.1 31.1 %all_gather.15 = f32[1,20,2048]{2,1,0:T(8,128)S(1)} all-gather(f32[1,20,256]{2,1,0:T(8,128)S(1)} %slice.5342), channel_id=1, replica_groups=mesh['section'=4,'obs'=8] {'obs'}, dimensions={2}, use_global_device_ids=true | all-gather | bytes 184320 | tf_op jit(solution)/shard_map/while/body/eval_jaxpr/all_gather | solution.py:144
  441.0 21.3 %psum.19 = f32[1,2]{1,0:T(1,128)S(1)} all-reduce(f32[1,2]{1,0:T(1,128)S(1)} %maximum_bitcast_fusion.6), channel_id=1, replica_groups=mesh['section'=4,'obs'=8] {'obs'}, use_global_device_ids=true, to_apply=%region_7.8 | all-reduce | flops 2 | bytes 16 | tf_op jit(solution)/shard_map/while/body/eval_jaxpr/psum | solution.py:156
  483.2 5.9 dynamic_update_slice.31
  499.5 31.2 %all_gather.15 = f32[1,20,2048]{2,1,0:T(8,128)S(1)} all-gather(f32[1,20,256]{2,1,0:T(8,128)S(1)} %slice.5342), channel_id=1, replica_groups=mesh['section'=4,'obs'=8] {'obs'}, dimensions={2}, use_global_device_ids=true | all-gather | bytes 184320 | tf_op jit(solution)/shard_map/while/body/eval_jaxpr/all_gather | solution.py:144
  537.4 21.4 %psum.19 = f32[1,2]{1,0:T(1,128)S(1)} all-reduce(f32[1,2]{1,0:T(1,128)S(1)} %maximum_bitcast_fusion.6), channel_id=1, replica_groups=mesh['section'=4,'obs'=8] {'obs'}, use_global_device_ids=true, to_apply=%region_7.8 | all-reduce | flops 2 | bytes 16 | tf_op jit(solution)/shard_map/while/body/eval_jaxpr/psum | solution.py:156
  579.8 5.9 dynamic_update_slice.31
  596.0 31.1 %all_gather.15 = f32[1,20,2048]{2,1,0:T(8,128)S(1)} all-gather(f32[1,20,256]{2,1,0:T(8,128)S(1)} %slice.5342), channel_id=1, replica_groups=mesh['section'=4,'obs'=8] {'obs'}, dimensions={2}, use_global_device_ids=true | all-gather | bytes 184320 | tf_op jit(solution)/shard_map/while/body/eval_jaxpr/all_gather | solution.py:144
  633.9 21.4 %psum.19 = f32[1,2]{1,0:T(1,128)S(1)} all-reduce(f32[1,2]{1,0:T(1,128)S(1)} %maximum_bitcast_fusion.6), channel_id=1, replica_groups=mesh['section'=4,'obs'=8] {'obs'}, use_global_device_ids=true, to_apply=%region_7.8 | all-reduce | flops 2 | bytes 16 | tf_op jit(solution)/shard_map/while/body/eval_jaxpr/psum | solution.py:156
  676.2 5.9 dynamic_update_slice.31
  (656 shorter events, 235.0 us)
Async XLA Ops:
  7.5 72.0 %all-to-all-start.1 = ((f32[1,8,8]{2,0,1:T(1,128)}), f32[1,8,8]{2,0,1:T(1,128)S(1)}, u32[]{:S(2)}, u32[]{:S(2)}) async-start(f32[1,8,8]{2,0,1:T(1,128)} %bitcast.2454), calls=%async_computation.1 | async-start | bytes 8192 | tf_op jit(solution)/shard_map/while/body/eval_jaxpr/all_to_all | solution.py:160
  79.5 10.2 %all-to-all-start = ((f32[1,8,8,230]{3,2,0,1:T(8,128)}), f32[1,8,8,230]{3,2,0,1:T(8,128)S(1)}, u32[]{:S(2)}, u32[]{:S(2)}) async-start(f32[1,8,8,230]{3,2,0,1:T(8,128)} %convolution_bitcast_fusion.4), calls=%async_computation | async-start | bytes 131072 | tf_op jit(solution)/shard_map/while/body/eval_jaxpr/all_to_all | solution.py:159
  93.4 0.7 copy-start.1
  95.9 7.6 %collective-permute-start = (f32[1,230,256]{2,1,0:T(8,128)S(1)}, f32[1,230,256]{2,1,0:T(8,128)S(1)}, u32[]{:S(2)}, u32[]{:S(2)}) collective-permute-start(f32[1,230,256]{2,1,0:T(8,128)S(1)} %pad_maximum_fusion.2), channel_id=1, source_target_pairs={{0,8},{8,16},{16,24},{1,9},{9,17},{17,25},{2,10},{10,18},{18,26},{... | collective-permute-start | bytes 706568 | tf_op jit(solution)/shard_map/while/body/eval_jaxpr/ppermute | solution.py:14
  108.1 67.8 %all-to-all-start.1 = ((f32[1,8,8]{2,0,1:T(1,128)}), f32[1,8,8]{2,0,1:T(1,128)S(1)}, u32[]{:S(2)}, u32[]{:S(2)}) async-start(f32[1,8,8]{2,0,1:T(1,128)} %bitcast.2454), calls=%async_computation.1 | async-start | bytes 8192 | tf_op jit(solution)/shard_map/while/body/eval_jaxpr/all_to_all | solution.py:160
  175.9 10.2 %all-to-all-start = ((f32[1,8,8,230]{3,2,0,1:T(8,128)}), f32[1,8,8,230]{3,2,0,1:T(8,128)S(1)}, u32[]{:S(2)}, u32[]{:S(2)}) async-start(f32[1,8,8,230]{3,2,0,1:T(8,128)} %convolution_bitcast_fusion.4), calls=%async_computation | async-start | bytes 131072 | tf_op jit(solution)/shard_map/while/body/eval_jaxpr/all_to_all | solution.py:159
  192.3 7.6 %collective-permute-start = (f32[1,230,256]{2,1,0:T(8,128)S(1)}, f32[1,230,256]{2,1,0:T(8,128)S(1)}, u32[]{:S(2)}, u32[]{:S(2)}) collective-permute-start(f32[1,230,256]{2,1,0:T(8,128)S(1)} %pad_maximum_fusion.2), channel_id=1, source_target_pairs={{0,8},{8,16},{16,24},{1,9},{9,17},{17,25},{2,10},{10,18},{18,26},{... | collective-permute-start | bytes 706568 | tf_op jit(solution)/shard_map/while/body/eval_jaxpr/ppermute | solution.py:14
  204.5 67.7 %all-to-all-start.1 = ((f32[1,8,8]{2,0,1:T(1,128)}), f32[1,8,8]{2,0,1:T(1,128)S(1)}, u32[]{:S(2)}, u32[]{:S(2)}) async-start(f32[1,8,8]{2,0,1:T(1,128)} %bitcast.2454), calls=%async_computation.1 | async-start | bytes 8192 | tf_op jit(solution)/shard_map/while/body/eval_jaxpr/all_to_all | solution.py:160
  272.2 10.2 %all-to-all-start = ((f32[1,8,8,230]{3,2,0,1:T(8,128)}), f32[1,8,8,230]{3,2,0,1:T(8,128)S(1)}, u32[]{:S(2)}, u32[]{:S(2)}) async-start(f32[1,8,8,230]{3,2,0,1:T(8,128)} %convolution_bitcast_fusion.4), calls=%async_computation | async-start | bytes 131072 | tf_op jit(solution)/shard_map/while/body/eval_jaxpr/all_to_all | solution.py:159
  288.6 7.6 %collective-permute-start = (f32[1,230,256]{2,1,0:T(8,128)S(1)}, f32[1,230,256]{2,1,0:T(8,128)S(1)}, u32[]{:S(2)}, u32[]{:S(2)}) collective-permute-start(f32[1,230,256]{2,1,0:T(8,128)S(1)} %pad_maximum_fusion.2), channel_id=1, source_target_pairs={{0,8},{8,16},{16,24},{1,9},{9,17},{17,25},{2,10},{10,18},{18,26},{... | collective-permute-start | bytes 706568 | tf_op jit(solution)/shard_map/while/body/eval_jaxpr/ppermute | solution.py:14
  300.9 67.9 %all-to-all-start.1 = ((f32[1,8,8]{2,0,1:T(1,128)}), f32[1,8,8]{2,0,1:T(1,128)S(1)}, u32[]{:S(2)}, u32[]{:S(2)}) async-start(f32[1,8,8]{2,0,1:T(1,128)} %bitcast.2454), calls=%async_computation.1 | async-start | bytes 8192 | tf_op jit(solution)/shard_map/while/body/eval_jaxpr/all_to_all | solution.py:160
  368.8 10.2 %all-to-all-start = ((f32[1,8,8,230]{3,2,0,1:T(8,128)}), f32[1,8,8,230]{3,2,0,1:T(8,128)S(1)}, u32[]{:S(2)}, u32[]{:S(2)}) async-start(f32[1,8,8,230]{3,2,0,1:T(8,128)} %convolution_bitcast_fusion.4), calls=%async_computation | async-start | bytes 131072 | tf_op jit(solution)/shard_map/while/body/eval_jaxpr/all_to_all | solution.py:159
  385.2 7.6 %collective-permute-start = (f32[1,230,256]{2,1,0:T(8,128)S(1)}, f32[1,230,256]{2,1,0:T(8,128)S(1)}, u32[]{:S(2)}, u32[]{:S(2)}) collective-permute-start(f32[1,230,256]{2,1,0:T(8,128)S(1)} %pad_maximum_fusion.2), channel_id=1, source_target_pairs={{0,8},{8,16},{16,24},{1,9},{9,17},{17,25},{2,10},{10,18},{18,26},{... | collective-permute-start | bytes 706568 | tf_op jit(solution)/shard_map/while/body/eval_jaxpr/ppermute | solution.py:14
  397.4 67.8 %all-to-all-start.1 = ((f32[1,8,8]{2,0,1:T(1,128)}), f32[1,8,8]{2,0,1:T(1,128)S(1)}, u32[]{:S(2)}, u32[]{:S(2)}) async-start(f32[1,8,8]{2,0,1:T(1,128)} %bitcast.2454), calls=%async_computation.1 | async-start | bytes 8192 | tf_op jit(solution)/shard_map/while/body/eval_jaxpr/all_to_all | solution.py:160
  465.2 10.2 %all-to-all-start = ((f32[1,8,8,230]{3,2,0,1:T(8,128)}), f32[1,8,8,230]{3,2,0,1:T(8,128)S(1)}, u32[]{:S(2)}, u32[]{:S(2)}) async-start(f32[1,8,8,230]{3,2,0,1:T(8,128)} %convolution_bitcast_fusion.4), calls=%async_computation | async-start | bytes 131072 | tf_op jit(solution)/shard_map/while/body/eval_jaxpr/all_to_all | solution.py:159
  481.6 7.6 %collective-permute-start = (f32[1,230,256]{2,1,0:T(8,128)S(1)}, f32[1,230,256]{2,1,0:T(8,128)S(1)}, u32[]{:S(2)}, u32[]{:S(2)}) collective-permute-start(f32[1,230,256]{2,1,0:T(8,128)S(1)} %pad_maximum_fusion.2), channel_id=1, source_target_pairs={{0,8},{8,16},{16,24},{1,9},{9,17},{17,25},{2,10},{10,18},{18,26},{... | collective-permute-start | bytes 706568 | tf_op jit(solution)/shard_map/while/body/eval_jaxpr/ppermute | solution.py:14
  493.8 67.9 %all-to-all-start.1 = ((f32[1,8,8]{2,0,1:T(1,128)}), f32[1,8,8]{2,0,1:T(1,128)S(1)}, u32[]{:S(2)}, u32[]{:S(2)}) async-start(f32[1,8,8]{2,0,1:T(1,128)} %bitcast.2454), calls=%async_computation.1 | async-start | bytes 8192 | tf_op jit(solution)/shard_map/while/body/eval_jaxpr/all_to_all | solution.py:160
  561.7 10.2 %all-to-all-start = ((f32[1,8,8,230]{3,2,0,1:T(8,128)}), f32[1,8,8,230]{3,2,0,1:T(8,128)S(1)}, u32[]{:S(2)}, u32[]{:S(2)}) async-start(f32[1,8,8,230]{3,2,0,1:T(8,128)} %convolution_bitcast_fusion.4), calls=%async_computation | async-start | bytes 131072 | tf_op jit(solution)/shard_map/while/body/eval_jaxpr/all_to_all | solution.py:159
  578.1 7.6 %collective-permute-start = (f32[1,230,256]{2,1,0:T(8,128)S(1)}, f32[1,230,256]{2,1,0:T(8,128)S(1)}, u32[]{:S(2)}, u32[]{:S(2)}) collective-permute-start(f32[1,230,256]{2,1,0:T(8,128)S(1)} %pad_maximum_fusion.2), channel_id=1, source_target_pairs={{0,8},{8,16},{16,24},{1,9},{9,17},{17,25},{2,10},{10,18},{18,26},{... | collective-permute-start | bytes 706568 | tf_op jit(solution)/shard_map/while/body/eval_jaxpr/ppermute | solution.py:14
  590.3 67.8 %all-to-all-start.1 = ((f32[1,8,8]{2,0,1:T(1,128)}), f32[1,8,8]{2,0,1:T(1,128)S(1)}, u32[]{:S(2)}, u32[]{:S(2)}) async-start(f32[1,8,8]{2,0,1:T(1,128)} %bitcast.2454), calls=%async_computation.1 | async-start | bytes 8192 | tf_op jit(solution)/shard_map/while/body/eval_jaxpr/all_to_all | solution.py:160
  658.1 10.2 %all-to-all-start = ((f32[1,8,8,230]{3,2,0,1:T(8,128)}), f32[1,8,8,230]{3,2,0,1:T(8,128)S(1)}, u32[]{:S(2)}, u32[]{:S(2)}) async-start(f32[1,8,8,230]{3,2,0,1:T(8,128)} %convolution_bitcast_fusion.4), calls=%async_computation | async-start | bytes 131072 | tf_op jit(solution)/shard_map/while/body/eval_jaxpr/all_to_all | solution.py:159
  674.5 7.6 %collective-permute-start = (f32[1,230,256]{2,1,0:T(8,128)S(1)}, f32[1,230,256]{2,1,0:T(8,128)S(1)}, u32[]{:S(2)}, u32[]{:S(2)}) collective-permute-start(f32[1,230,256]{2,1,0:T(8,128)S(1)} %pad_maximum_fusion.2), channel_id=1, source_target_pairs={{0,8},{8,16},{16,24},{1,9},{9,17},{17,25},{2,10},{10,18},{18,26},{... | collective-permute-start | bytes 706568 | tf_op jit(solution)/shard_map/while/body/eval_jaxpr/ppermute | solution.py:14
  682.1 0.9 copy-start.2
  682.2 0.9 copy-start.3
  (23 other events, 15.4 us)
where the time goes:
time: 692 us; the launch traced here: 683 us
  blocking collectives  367 us (53%)
  local copies, waits for them, and re-layouts  109 us (16%)
  other arithmetic  68.2 us (10%)
  starting transfers between devices  59.8 us (9%)
  waiting for transfers between devices  38.9 us (6%)
  loops' own time  25.7 us (4%)
  matrix products  12.9 us (2%)
    all_gather x7, blocking collectives, window_work(): all_coeffs = lax.all_gather(beta_prior, 'obs', axis=2, tiled=True)  218 us
    psum x7, blocking collectives, window_work(): totals = lax.psum(statistics, 'obs')  150 us
    dynamic_update_slice x28, local copies, waits for them, and re-layouts, store_entry(): return lax.dynamic_update_slice_in_dim(buffer, updated, slot_index, 1)  43.8 us
    all_to_all x7, waiting for transfers between devices, window_work(): lax.all_to_all(send_rows, 'obs', split_axis=1, concat_axis=1, tiled=True)  38.9 us
    all_to_all x7, starting transfers between devices, window_work(): lax.all_to_all(send_channel, 'obs', split_axis=1, concat_axis=1, tiled=True)  27.2 us
    another operation x1, loops' own time, local(): lax.fori_loop(0, stream_count + section_count - 1, tick_step, initial)  25.7 us
    all_to_all x7, starting transfers between devices, window_work(): lax.all_to_all(send_rows, 'obs', split_axis=1, concat_axis=1, tiled=True)  23.5 us
  transfers between devices with their start and end apart: 21, of which 7 were waited for; matrix products, arithmetic and copies ran while one was open for 19% of the time, Pallas kernels for 0%

commit v1 on v0

v1 whole, which is shorter than its diff:
```python
import jax
import jax.numpy as jnp
import numpy as np
from jax import lax
from jax.sharding import PartitionSpec as P

HUBER_SQ = 9.0
PRIOR_WEIGHT = 64.0


def upper_positions(dimension):
    return np.array(
        [i * dimension + j for i in range(dimension) for j in range(i, dimension)], dtype=np.int32
    )


def solve_packed(packed, target):
    dimension = target.shape[0]
    placing = {}
    counter = 0
    for i in range(dimension):
        for j in range(i, dimension):
            placing[i, j] = counter
            counter += 1
    factor = [[None] * dimension for i in range(dimension)]
    for j in range(dimension):
        pivot_root = jnp.sqrt(
            packed[placing[j, j]] - sum((factor[j][k] * factor[j][k] for k in range(j)))
        )
        factor[j][j] = pivot_root
        for i in range(j + 1, dimension):
            factor[i][j] = (
                packed[placing[j, i]] - sum((factor[i][k] * factor[j][k] for k in range(j)))
            ) / pivot_root
    forward = []
    for i in range(dimension):
        forward.append(
            (target[i] - sum((factor[i][k] * forward[k] for k in range(i)))) / factor[i][i]
        )
    backward = [None] * dimension
    for i in reversed(range(dimension)):
        backward[i] = (
            forward[i] - sum((factor[k][i] * backward[k] for k in range(i + 1, dimension)))
        ) / factor[i][i]
    return jnp.stack(backward)


def block_rows(fields, block_coeffs, pred_count):
    block_count = block_coeffs.shape[1]
    row_count = fields.shape[1]
    block_width = row_count // block_count
    upper_index = upper_positions(pred_count)
    shaped = fields[:pred_count].reshape(pred_count, block_count, block_width)
    departed = fields[pred_count].reshape(block_count, block_width)
    scale_row = fields[pred_count + 1].reshape(block_count, block_width)
    offset = jnp.sum(shaped * block_coeffs[:, :, None], axis=0)
    residual = departed - offset
    weight = scale_row / (1.0 + scale_row * residual * residual / HUBER_SQ)
    weighted = lax.reduce_precision(weight[None] * shaped, 8, 7)
    chi_square = jnp.sum(weight * residual * residual)
    passed_count = jnp.sum((scale_row > 0.0).astype(jnp.float32))
    gram_full = lax.dot_general(
        weighted, shaped, (((2,), (2,)), ((1,), (1,))), preferred_element_type=jnp.float32
    )
    gram_upper = gram_full.reshape(block_count, pred_count * pred_count)[:, upper_index]
    gradient = jnp.sum(weighted * residual[None], axis=2).T
    return (jnp.concatenate([gram_upper, gradient], axis=1), jnp.stack([chi_square, passed_count]))


def local(
    predictors,
    departures,
    obs_precision,
    qc_pass,
    block_channel,
    stream_order,
    prior_coeffs,
    prior_info,
    memory_factor,
):
    sections = lax.axis_size("section")
    owners = lax.axis_size("obs")
    section_place = lax.axis_index("section")
    stream_count = stream_order.shape[0]
    local_channels = memory_factor.shape[0]
    block_count = block_channel.shape[2]
    pred_count = prior_coeffs.shape[1]
    tri_count = prior_info.shape[1]
    column_count = tri_count + pred_count
    capacity = 2 * block_count // owners
    slots = owners * capacity
    highest = lax.Precision.HIGHEST
    groups = -(-stream_count // sections)

    def turn(array, axis):
        return lax.all_to_all(array, axis, split_axis=0, concat_axis=0, tiled=True)

    def select_rows(hot, values, dims):
        return lax.dot_general(
            hot, values, (dims, ((), ())), precision=highest, preferred_element_type=jnp.float32
        )

    coeff_parts = []
    info_parts = []
    for group in range(groups):
        wanted = np.minimum(np.arange(sections) + group * sections, stream_count - 1)
        streams = stream_order[wanted]
        own_stream = stream_order[jnp.minimum(section_place + group * sections, stream_count - 1)]
        kept = jnp.take(obs_precision[0] * qc_pass[0].astype(jnp.float32), streams, axis=0)
        fields = jnp.concatenate(
            [
                jnp.take(predictors[0], streams, axis=0).astype(jnp.float32),
                jnp.take(departures[0], streams, axis=0)[:, None],
                kept[:, None],
            ],
            axis=1,
        )
        channel = turn(jnp.take(block_channel[0], streams, axis=0), "section")
        fields = turn(fields, "section")
        owner_index = channel // local_channels
        owner_hot = (owner_index[:, :, None] == jnp.arange(owners)).astype(jnp.int32)
        ranking = jnp.sum((jnp.cumsum(owner_hot, axis=1) - 1) * owner_hot, axis=2)
        slot_of = owner_index * capacity + ranking
        is_slot = slot_of[:, :, None] == jnp.arange(slots, dtype=jnp.int32)
        placing = is_slot.astype(jnp.float32)
        asked = jnp.sum(jnp.where(is_slot, (channel % local_channels)[:, :, None] + 1, 0), axis=1) - 1
        asked = asked.reshape(sections, owners, capacity).swapaxes(0, 1)
        asked = turn(asked, "obs").swapaxes(0, 1).reshape(sections, slots)
        asked_hot = (asked[:, :, None] == jnp.arange(local_channels)).astype(jnp.float32)

        beta = lax.dynamic_index_in_dim(prior_coeffs, own_stream, 0, keepdims=False)
        kept_info = lax.dynamic_index_in_dim(prior_info, own_stream, 0, keepdims=False)
        results = []
        for w in range(sections):
            sent = select_rows(asked_hot[w], beta, ((1,), (1,)))
            got = turn(sent.reshape(owners, capacity, pred_count), "obs")
            block_coeffs = select_rows(got.reshape(slots, pred_count), placing[w], ((0,), (1,)))
            block_sums, statistics = block_rows(fields[w], block_coeffs, pred_count)
            rows = select_rows(placing[w], block_sums, ((0,), (0,)))
            rows = jnp.concatenate(
                [rows, jnp.broadcast_to(statistics[None], (slots, 2))], axis=1
            ).reshape(owners, capacity, column_count + 2)
            rows = turn(rows, "obs")
            totals = jnp.sum(rows[:, 0, column_count:], axis=0)
            inflation = (totals[0] + PRIOR_WEIGHT) / (totals[1] + PRIOR_WEIGHT)
            normal = (
                select_rows(
                    rows.reshape(slots, column_count + 2)[:, :column_count],
                    asked_hot[w],
                    ((0,), (0,)),
                )
                / inflation
            )
            info_post = kept_info + normal[:tri_count]
            beta = beta + solve_packed(info_post, normal[tri_count:])
            kept_info = memory_factor[None] * info_post
            results.append(jnp.concatenate([beta, info_post], axis=0))
        landed = turn(jnp.stack(results), "section")
        count = min(sections, stream_count - group * sections)
        coeff_parts.append(landed[:count, :pred_count])
        info_parts.append(landed[:count, pred_count:])
    if groups == 1:
        return (coeff_parts[0][None], info_parts[0][None])
    return (jnp.concatenate(coeff_parts)[None], jnp.concatenate(info_parts)[None])


def solution(mesh):
    in_specs = (
        P("section", None, None, "obs"),
        P("section", None, "obs"),
        P("section", None, "obs"),
        P("section", None, "obs"),
        P("section", None, "obs"),
        P(),
        P(None, None, "obs"),
        P(None, None, "obs"),
        P("obs"),
    )
    out_specs = (P("section", None, None, "obs"), P("section", None, None, "obs"))
    return jax.shard_map(local, mesh=mesh, in_specs=in_specs, out_specs=out_specs, check_vma=False)
```

time: 692 us -> 213 us (0.31); the launches traced: 683 us -> 212 us
  blocking collectives: 367 us -> 61 us
  local copies, waits for them, and re-layouts: 109 us -> 31.9 us
  starting transfers between devices: 59.8 us -> 24.2 us
  other arithmetic: 68.2 us -> 36.2 us
  loops' own time: 25.7 us -> 0 us
  between operations: 0.72 us -> 10.2 us
    all_gather x7 -> x0, blocking collectives: 218 us -> none  [window_work(): all_coeffs = lax.all_gather(beta_prior, 'obs', axis=2, tiled=True)]
    psum x7 -> x0, blocking collectives: 150 us -> none  [window_work(): totals = lax.psum(statistics, 'obs')]
    all_to_all x0 -> x6, blocking collectives: none -> 61 us  [turn(): return lax.all_to_all(array, axis, split_axis=0, concat_axis=0, tiled=True)]
    dynamic_update_slice x28 -> x0, local copies, waits for them, and re-layouts: 43.8 us -> none  [store_entry(): return lax.dynamic_update_slice_in_dim(buffer, updated, slot_index, 1)]
    all_to_all x14 -> x6, starting transfers between devices: 50.7 us -> 24.2 us  [turn(): return lax.all_to_all(array, axis, split_axis=0, concat_axis=0, tiled=True)]
    another operation x1 -> x0, loops' own time: 25.7 us -> none  [local(): lax.fori_loop(0, stream_count + section_count - 1, tick_step, initial)]
    gather x42 -> x13, local copies, waits for them, and re-layouts: 25.9 us -> 8.33 us  [the longest x8 3.09 us: block_rows(): gram_full.reshape(block_count, pred_count * pred_count)[:, upper_index]]
    reduce_sum x35 -> x14, other arithmetic: 19.2 us -> 4.76 us  [the longest x4 2.84 us: block_rows(): chi_square = jnp.sum(weight * residual * residual)]
  transfers between devices with their start and end apart: 21 -> 6, of which waited for: 7 -> 5; matrix products, arithmetic and copies ran while one was open for 19% -> 6% of each run, Pallas kernels for 0% -> 0%
where the time goes in v1:
time: 213 us; the launch traced here: 212 us
  blocking collectives  61 us (29%)
  waiting for transfers between devices  38.9 us (18%)
  other arithmetic  36.2 us (17%)
  local copies, waits for them, and re-layouts  31.9 us (15%)
  starting transfers between devices  24.2 us (11%)
  between operations  10.2 us (5%)
  matrix products  9.35 us (4%)
    all_to_all x6, blocking collectives, turn(): return lax.all_to_all(array, axis, split_axis=0, concat_axis=0, tiled=True)  61 us
    all_to_all x6, waiting for transfers between devices, turn(): return lax.all_to_all(array, axis, split_axis=0, concat_axis=0, tiled=True)  38.9 us
    all_to_all x6, starting transfers between devices, turn(): return lax.all_to_all(array, axis, split_axis=0, concat_axis=0, tiled=True)  24.2 us
    div x8, other arithmetic, solve_packed(): (target[i] - sum((factor[i][k] * forward[k] for k in range(i)))) / factor...  7.68 us
    dot_general x16, matrix products, select_rows(): lax.dot_general(hot, values, (dims, ((), ())), precision=highest, preferr...  7.47 us
    another operation x7, local copies, waits for them, and re-layouts, solve_packed(): return jnp.stack(backward)  6.79 us
    div x12, other arithmetic, solve_packed(): (forward[i] - sum((factor[k][i] * backward[k] for k in range(i + 1, dimen...  5.95 us
    another operation x4, other arithmetic, block_rows(): jnp.stack([chi_square, passed_count])  5.27 us
  transfers between devices with their start and end apart: 6, of which 5 were waited for; matrix products, arithmetic and copies ran while one was open for 6% of the time, Pallas kernels for 0%

profile of v1, /device:TPU:0, one launch (start us, length us, event | category | flops | bytes accessed | tf_op | source)
XLA Modules:
  0.0 211.8 jit_solution(8554238158894397909)
XLA Ops:
  0.7 1.4 gather_fusion
  4.0 4.2 %all-to-all-start = ((s32[4,1,32]{2,1,0:T(1,128)}), s32[4,1,32]{2,1,0:T(1,128)S(1)}, u32[]{:S(2)}, u32[]{:S(2)}) async-start(s32[4,1,32]{2,1,0:T(1,128)} %bitcast.6), calls=%async_computation | async-start | bytes 4096 | tf_op jit(solution)/shard_map/all_to_all | solution.py:96
  8.3 1.4 gather_fusion.7
  16.6 6.3 %all-to-all-start.2 = ((s32[8,4,8]{2,1,0:T(4,128)}), s32[8,4,8]{2,1,0:T(4,128)S(1)}, u32[]{:S(2)}, u32[]{:S(2)}) async-start(s32[8,4,8]{2,1,0:T(4,128)} %copy.138), calls=%async_computation.2 | async-start | bytes 32768 | tf_op jit(solution)/shard_map/all_to_all | solution.py:96
  23.9 5.6 %all-to-all-done.2 = s32[8,4,8]{2,1,0:T(4,128)S(1)} async-done(((s32[8,4,8]{2,1,0:T(4,128)}), s32[8,4,8]{2,1,0:T(4,128)S(1)}, u32[]{:S(2)}, u32[]{:S(2)}) %all-to-all-start.2) | async-done | bytes 1056 | tf_op jit(solution)/shard_map/all_to_all | solution.py:96
  30.5 3.3 %all-to-all-start.3 = ((f32[8,1,160]{2,1,0:T(1,128)}), f32[8,1,160]{2,1,0:T(1,128)S(1)}, u32[]{:S(2)}, u32[]{:S(2)}) async-start(f32[8,1,160]{2,1,0:T(1,128)} %reshape.695), calls=%async_computation.3 | async-start | bytes 16384 | tf_op jit(solution)/shard_map/all_to_all | solution.py:96
  33.9 1.3 pad_maximum_fusion
  35.2 5.1 %all-to-all-done.3 = f32[8,1,160]{2,1,0:T(1,128)S(1)} async-done(((f32[8,1,160]{2,1,0:T(1,128)}), f32[8,1,160]{2,1,0:T(1,128)S(1)}, u32[]{:S(2)}, u32[]{:S(2)}) %all-to-all-start.3) | async-done | bytes 5152 | tf_op jit(solution)/shard_map/all_to_all | solution.py:96
  40.3 3.6 %all-to-all-start.1 = ((f32[4,22,4096]{2,1,0:T(8,128)}), f32[4,22,4096]{2,1,0:T(8,128)S(1)}, u32[]{:S(2)}, u32[]{:S(2)}) async-start(f32[4,22,4096]{2,1,0:T(8,128)} %pad_maximum_fusion), calls=%async_computation.1 | async-start | bytes 3145728 | tf_op jit(solution)/shard_map/all_to_all | solution.py:96
  45.8 18.2 %all-to-all-done.1 = f32[4,22,4096]{2,1,0:T(8,128)S(1)} async-done(((f32[4,22,4096]{2,1,0:T(8,128)}), f32[4,22,4096]{2,1,0:T(8,128)S(1)}, u32[]{:S(2)}, u32[]{:S(2)}) %all-to-all-start.1) | async-done | bytes 1441824 | tf_op jit(solution)/shard_map/all_to_all | solution.py:96
  68.7 3.4 %all-to-all-start.4 = ((f32[8,8,232]{2,1,0:T(8,128)}), f32[8,8,232]{2,1,0:T(8,128)S(1)}, u32[]{:S(2)}, u32[]{:S(2)}) async-start(f32[8,8,232]{2,1,0:T(8,128)} %maximum_bitcast_fusion.4), calls=%async_computation.4 | async-start | bytes 131072 | tf_op jit(solution)/shard_map/all_to_all | solution.py:96
  72.2 6.6 %all-to-all-done.4 = f32[8,8,232]{2,1,0:T(8,128)S(1)} async-done(((f32[8,8,232]{2,1,0:T(8,128)}), f32[8,8,232]{2,1,0:T(8,128)S(1)}, u32[]{:S(2)}, u32[]{:S(2)}) %all-to-all-start.4) | async-done | bytes 59424 | tf_op jit(solution)/shard_map/all_to_all | solution.py:96
  87.1 8.9 %all_to_all.64 = f32[8,1,160]{2,1,0:T(1,128)S(1)} all-to-all(f32[8,1,160]{2,1,0:T(1,128)S(1)} %reshape.697), channel_id=1, replica_groups=mesh['section'=4,'obs'=8] {'obs'}, dimensions={0} | all-to-all | bytes 10240 | tf_op jit(solution)/shard_map/all_to_all | solution.py:96
  100.1 1.4 pad_maximum_fusion.4
  101.5 9.3 %all_to_all.65 = f32[8,8,232]{2,1,0:T(8,128)S(1)} all-to-all(f32[8,8,232]{2,1,0:T(8,128)S(1)} %maximum_bitcast_fusion.5), channel_id=1, replica_groups=mesh['section'=4,'obs'=8] {'obs'}, dimensions={0} | all-to-all | bytes 118784 | tf_op jit(solution)/shard_map/all_to_all | solution.py:96
  120.6 8.9 %all_to_all.66 = f32[8,1,160]{2,1,0:T(1,128)S(1)} all-to-all(f32[8,1,160]{2,1,0:T(1,128)S(1)} %reshape.699), channel_id=1, replica_groups=mesh['section'=4,'obs'=8] {'obs'}, dimensions={0} | all-to-all | bytes 10240 | tf_op jit(solution)/shard_map/all_to_all | solution.py:96
  137.9 9.3 %all_to_all.67 = f32[8,8,232]{2,1,0:T(8,128)S(1)} all-to-all(f32[8,8,232]{2,1,0:T(8,128)S(1)} %maximum_bitcast_fusion.6), channel_id=1, replica_groups=mesh['section'=4,'obs'=8] {'obs'}, dimensions={0} | all-to-all | bytes 118784 | tf_op jit(solution)/shard_map/all_to_all | solution.py:96
  155.9 2.2 %stack.423 = f32[1,20,256]{2,1,0:T(8,128)S(1)} concatenate(f32[1,1,256]{2,1,0:T(1,128)} %bitcast.1317, f32[1,1,256]{2,1,0:T(1,128)} %bitcast.1319, f32[1,1,256]{2,1,0:T(1,128)} %bitcast.1321, f32[1,1,256]{2,1,0:T(1,128)} %bitcast.1323, f32[1,1,256]{2,1,0:T(1,128)} %bitcast.1325, f32[1,1,256]{2,1,0:T(1,128)} %bitcast.1327, f32[1,1,256]{2,1,0:T(1,128)} %bitcast.1329, ...), dimensions={1} | concatenate | bytes 40960 | tf_op jit(solution)/shard_map/stack | solution.py:45
  159.1 8.9 %all_to_all.68 = f32[8,1,160]{2,1,0:T(1,128)S(1)} all-to-all(f32[8,1,160]{2,1,0:T(1,128)S(1)} %reshape.701), channel_id=1, replica_groups=mesh['section'=4,'obs'=8] {'obs'}, dimensions={0} | all-to-all | bytes 10240 | tf_op jit(solution)/shard_map/all_to_all | solution.py:96
  175.9 3.4 %all-to-all-start.10 = ((f32[8,8,232]{2,1,0:T(8,128)}), f32[8,8,232]{2,1,0:T(8,128)S(1)}, u32[]{:S(2)}, u32[]{:S(2)}) async-start(f32[8,8,232]{2,1,0:T(8,128)} %maximum_bitcast_fusion.7), calls=%async_computation.10 | async-start | bytes 131072 | tf_op jit(solution)/shard_map/all_to_all | solution.py:96
  179.3 2.1 %stack.335 = f32[20,256]{1,0:T(8,128)S(1)} concatenate(f32[1,256]{1,0:T(1,128)S(1)} %bitcast.1264, f32[1,256]{1,0:T(1,128)S(1)} %bitcast.1266, f32[1,256]{1,0:T(1,128)S(1)} %bitcast.1268, f32[1,256]{1,0:T(1,128)S(1)} %bitcast.1270, f32[1,256]{1,0:T(1,128)S(1)} %bitcast.1272, f32[1,256]{1,0:T(1,128)} %bitcast.1274, f32[1,256]{1,0:T(1,128)} %bitcast.1276, f32[1,256]{1,0:T(1,128)} %copy-done.10, ...), dimensions={0} | concatenate | bytes 40960 | tf_op jit(solution)/shard_map/stack | solution.py:45
  182.6 3.5 %all-to-all-done.10 = f32[8,8,232]{2,1,0:T(8,128)S(1)} async-done(((f32[8,8,232]{2,1,0:T(8,128)}), f32[8,8,232]{2,1,0:T(8,128)S(1)}, u32[]{:S(2)}, u32[]{:S(2)}) %all-to-all-start.10) | async-done | bytes 59424 | tf_op jit(solution)/shard_map/all_to_all | solution.py:96
  191.4 1.7 subtract_divide_fusion.30
  194.0 15.8 %all_to_all.69 = f32[4,230,256]{2,1,0:T(8,128)S(1)} all-to-all(f32[4,230,256]{2,1,0:T(8,128)S(1)} %pad_maximum_fusion.1), channel_id=1, replica_groups=mesh['section'=4,'obs'=8] {'section'}, dimensions={0} | all-to-all | bytes 1884160 | tf_op jit(solution)/shard_map/all_to_all | solution.py:96
  (393 shorter events, 66.0 us)
Async XLA Ops:
  0.6 71.4 %copy-start = (f32[4,210,256]{2,0,1:T(4,128)S(1)}, f32[4,210,256]{2,0,1:T(4,128)}, u32[]{:S(2)}) copy-start(f32[4,210,256]{2,0,1:T(4,128)} %param.28) | copy-start | bytes 2580484
  4.0 11.3 %all-to-all-start = ((s32[4,1,32]{2,1,0:T(1,128)}), s32[4,1,32]{2,1,0:T(1,128)S(1)}, u32[]{:S(2)}, u32[]{:S(2)}) async-start(s32[4,1,32]{2,1,0:T(1,128)} %bitcast.6), calls=%async_computation | async-start | bytes 4096 | tf_op jit(solution)/shard_map/all_to_all | solution.py:96
  16.6 12.9 %all-to-all-start.2 = ((s32[8,4,8]{2,1,0:T(4,128)}), s32[8,4,8]{2,1,0:T(4,128)S(1)}, u32[]{:S(2)}, u32[]{:S(2)}) async-start(s32[8,4,8]{2,1,0:T(4,128)} %copy.138), calls=%async_computation.2 | async-start | bytes 32768 | tf_op jit(solution)/shard_map/all_to_all | solution.py:96
  29.7 57.2 %copy-start.3 = (pred[4,64,256]{2,1,0:T(32,128)(4,1)}, pred[4,64,256]{2,1,0:T(32,128)(4,1)S(1)}, u32[]{:S(2)}) copy-start(pred[4,64,256]{2,1,0:T(32,128)(4,1)S(1)} %iota_compare_fusion) | copy-start | bytes 196612
  30.5 9.8 %all-to-all-start.3 = ((f32[8,1,160]{2,1,0:T(1,128)}), f32[8,1,160]{2,1,0:T(1,128)S(1)}, u32[]{:S(2)}, u32[]{:S(2)}) async-start(f32[8,1,160]{2,1,0:T(1,128)} %reshape.695), calls=%async_computation.3 | async-start | bytes 16384 | tf_op jit(solution)/shard_map/all_to_all | solution.py:96
  40.3 23.6 %all-to-all-start.1 = ((f32[4,22,4096]{2,1,0:T(8,128)}), f32[4,22,4096]{2,1,0:T(8,128)S(1)}, u32[]{:S(2)}, u32[]{:S(2)}) async-start(f32[4,22,4096]{2,1,0:T(8,128)} %pad_maximum_fusion), calls=%async_computation.1 | async-start | bytes 3145728 | tf_op jit(solution)/shard_map/all_to_all | solution.py:96
  68.7 10.2 %all-to-all-start.4 = ((f32[8,8,232]{2,1,0:T(8,128)}), f32[8,8,232]{2,1,0:T(8,128)S(1)}, u32[]{:S(2)}, u32[]{:S(2)}) async-start(f32[8,8,232]{2,1,0:T(8,128)} %maximum_bitcast_fusion.4), calls=%async_computation.4 | async-start | bytes 131072 | tf_op jit(solution)/shard_map/all_to_all | solution.py:96
  98.5 15.4 %copy-start.4 = (f32[256]{0:T(256)S(1)}, f32[256]{0:T(256)}, u32[]{:S(2)}) copy-start(f32[256]{0:T(256)} %param.29) | copy-start | bytes 3076
  118.7 13.8 %copy-start.32 = (f32[1,256]{1,0:T(1,128)}, f32[1,256]{1,0:T(1,128)S(1)}, u32[]{:S(2)}) copy-start(f32[1,256]{1,0:T(1,128)S(1)} %get-tuple-element.982) | copy-start | bytes 3076
  118.7 13.8 %copy-start.34 = (f32[1,256]{1,0:T(1,128)}, f32[1,256]{1,0:T(1,128)S(1)}, u32[]{:S(2)}) copy-start(f32[1,256]{1,0:T(1,128)S(1)} %get-tuple-element.983) | copy-start | bytes 3076
  118.7 13.8 %copy-start.36 = (f32[1,256]{1,0:T(1,128)}, f32[1,256]{1,0:T(1,128)S(1)}, u32[]{:S(2)}) copy-start(f32[1,256]{1,0:T(1,128)S(1)} %get-tuple-element.984) | copy-start | bytes 3076
  118.7 13.8 %copy-start.38 = (f32[1,256]{1,0:T(1,128)}, f32[1,256]{1,0:T(1,128)S(1)}, u32[]{:S(2)}) copy-start(f32[1,256]{1,0:T(1,128)S(1)} %get-tuple-element.985) | copy-start | bytes 3076
  118.8 13.8 %copy-start.40 = (f32[1,256]{1,0:T(1,128)}, f32[1,256]{1,0:T(1,128)S(1)}, u32[]{:S(2)}) copy-start(f32[1,256]{1,0:T(1,128)S(1)} %get-tuple-element.986) | copy-start | bytes 3076
  118.8 13.8 %copy-start.42 = (f32[1,256]{1,0:T(1,128)}, f32[1,256]{1,0:T(1,128)S(1)}, u32[]{:S(2)}) copy-start(f32[1,256]{1,0:T(1,128)S(1)} %get-tuple-element.987) | copy-start | bytes 3076
  118.8 13.8 %copy-start.44 = (f32[1,256]{1,0:T(1,128)}, f32[1,256]{1,0:T(1,128)S(1)}, u32[]{:S(2)}) copy-start(f32[1,256]{1,0:T(1,128)S(1)} %get-tuple-element.988) | copy-start | bytes 3076
  118.8 13.8 %copy-start.46 = (f32[1,256]{1,0:T(1,128)}, f32[1,256]{1,0:T(1,128)S(1)}, u32[]{:S(2)}) copy-start(f32[1,256]{1,0:T(1,128)S(1)} %get-tuple-element.989) | copy-start | bytes 3076
  118.8 13.8 %copy-start.48 = (f32[1,256]{1,0:T(1,128)}, f32[1,256]{1,0:T(1,128)S(1)}, u32[]{:S(2)}) copy-start(f32[1,256]{1,0:T(1,128)S(1)} %get-tuple-element.990) | copy-start | bytes 3076
  118.8 13.8 %copy-start.50 = (f32[1,256]{1,0:T(1,128)}, f32[1,256]{1,0:T(1,128)S(1)}, u32[]{:S(2)}) copy-start(f32[1,256]{1,0:T(1,128)S(1)} %get-tuple-element.991) | copy-start | bytes 3076
  118.8 13.8 %copy-start.52 = (f32[1,256]{1,0:T(1,128)}, f32[1,256]{1,0:T(1,128)S(1)}, u32[]{:S(2)}) copy-start(f32[1,256]{1,0:T(1,128)S(1)} %get-tuple-element.992) | copy-start | bytes 3076
  155.9 15.1 %copy-start.63 = (f32[1,256]{1,0:T(1,128)}, f32[1,256]{1,0:T(1,128)S(1)}, u32[]{:S(2)}) copy-start(f32[1,256]{1,0:T(1,128)S(1)} %get-tuple-element.505) | copy-start | bytes 3076
  155.9 15.1 %copy-start.65 = (f32[1,256]{1,0:T(1,128)}, f32[1,256]{1,0:T(1,128)S(1)}, u32[]{:S(2)}) copy-start(f32[1,256]{1,0:T(1,128)S(1)} %get-tuple-element.506) | copy-start | bytes 3076
  155.9 15.1 %copy-start.67 = (f32[1,256]{1,0:T(1,128)}, f32[1,256]{1,0:T(1,128)S(1)}, u32[]{:S(2)}) copy-start(f32[1,256]{1,0:T(1,128)S(1)} %get-tuple-element.507) | copy-start | bytes 3076
  155.9 15.1 %copy-start.69 = (f32[1,256]{1,0:T(1,128)}, f32[1,256]{1,0:T(1,128)S(1)}, u32[]{:S(2)}) copy-start(f32[1,256]{1,0:T(1,128)S(1)} %get-tuple-element.508) | copy-start | bytes 3076
  175.9 10.2 %all-to-all-start.10 = ((f32[8,8,232]{2,1,0:T(8,128)}), f32[8,8,232]{2,1,0:T(8,128)S(1)}, u32[]{:S(2)}, u32[]{:S(2)}) async-start(f32[8,8,232]{2,1,0:T(8,128)} %maximum_bitcast_fusion.7), calls=%async_computation.10 | async-start | bytes 131072 | tf_op jit(solution)/shard_map/all_to_all | solution.py:96
  (59 other events, 586.3 us)

commit v2 on v1

--- a/solution.py
+++ b/solution.py
@@ -2,6 +2,8 @@
 import jax.numpy as jnp
 import numpy as np
 from jax import lax
+from jax.experimental import pallas as pl
+from jax.experimental.pallas import tpu as pltpu
 from jax.sharding import PartitionSpec as P
 
 HUBER_SQ = 9.0
@@ -14,35 +16,63 @@
     )
 
 
-def solve_packed(packed, target):
-    dimension = target.shape[0]
-    placing = {}
-    counter = 0
-    for i in range(dimension):
-        for j in range(i, dimension):
-            placing[i, j] = counter
-            counter += 1
-    factor = [[None] * dimension for i in range(dimension)]
+def update_kernel(normal_ref, kept_ref, beta_ref, inflation_ref, result_ref, factor_ref, work_ref):
+    dimension = beta_ref.shape[0]
+    tri_count = kept_ref.shape[0]
+    padded, channels = work_ref.shape
+    inverse = 1.0 / inflation_ref[0, 0]
+    info = kept_ref[...] + normal_ref[pl.ds(0, tri_count), :] * inverse
+    result_ref[pl.ds(dimension, tri_count), :] = info
+    work_ref[pl.ds(0, dimension), :] = normal_ref[pl.ds(tri_count, dimension), :] * inverse
+    start = 0
     for j in range(dimension):
-        pivot_root = jnp.sqrt(
-            packed[placing[j, j]] - sum((factor[j][k] * factor[j][k] for k in range(j)))
-        )
-        factor[j][j] = pivot_root
-        for i in range(j + 1, dimension):
-            factor[i][j] = (
-                packed[placing[j, i]] - sum((factor[i][k] * factor[j][k] for k in range(j)))
-            ) / pivot_root
+        length = dimension - j
+        factor_ref[j, pl.ds(j, length), :] = result_ref[pl.ds(dimension + start, length), :]
+        start += length
+    roots = []
     forward = []
-    for i in range(dimension):
-        forward.append(
-            (target[i] - sum((factor[i][k] * forward[k] for k in range(i)))) / factor[i][i]
-        )
-    backward = [None] * dimension
+    for j in range(dimension):
+        low = 8 * (j // 8)
+        high = padded - low
+        column = factor_ref[j, pl.ds(low, high), :]
+        for k in range(j):
+            column = column - factor_ref[k, pl.ds(low, high), :] * factor_ref[k, pl.ds(j, 1), :]
+        inverse_root = 1.0 / jnp.sqrt(column[j - low : j - low + 1, :])
+        column = column * inverse_root
+        factor_ref[j, pl.ds(low, high), :] = column
+        target = work_ref[pl.ds(low, high), :]
+        solved = target[j - low : j - low + 1, :] * inverse_root
+        work_ref[pl.ds(low, high), :] = target - column * solved
+        roots.append(inverse_root)
+        forward.append(solved)
+    line = lax.broadcasted_iota(jnp.int32, (padded, channels), 0)
+    answer = jnp.zeros((padded, channels), jnp.float32)
     for i in reversed(range(dimension)):
-        backward[i] = (
-            forward[i] - sum((factor[k][i] * backward[k] for k in range(i + 1, dimension)))
-        ) / factor[i][i]
-    return jnp.stack(backward)
+        low = 8 * (i // 8)
+        high = padded - low
+        places = line[low:, :]
+        below = jnp.logical_and(places > i, places < dimension)
+        terms = jnp.where(below, factor_ref[i, pl.ds(low, high), :] * answer[low:, :], 0.0)
+        value = (forward[i] - jnp.sum(terms, axis=0, keepdims=True)) * roots[i]
+        answer = jnp.where(line == i, value, answer)
+    result_ref[pl.ds(0, dimension), :] = beta_ref[...] + answer[:dimension, :]
+
+
+def update_state(normal, kept_info, beta, inflation):
+    dimension, channels = beta.shape
+    padded = -(-dimension // 8) * 8
+    whole = pl.BlockSpec(memory_space=pltpu.VMEM)
+    return pl.pallas_call(
+        update_kernel,
+        out_shape=jax.ShapeDtypeStruct(normal.shape, jnp.float32),
+        in_specs=[whole, whole, whole, pl.BlockSpec(memory_space=pltpu.SMEM)],
+        out_specs=whole,
+        scratch_shapes=[
+            pltpu.VMEM((dimension, padded, channels), jnp.float32),
+            pltpu.VMEM((padded, channels), jnp.float32),
+        ],
+        name="update_state",
+    )(normal, kept_info, beta, inflation.reshape(1, 1))
 
 
 def block_rows(fields, block_coeffs, pred_count):
@@ -116,7 +146,15 @@
             axis=1,
         )
         channel = turn(jnp.take(block_channel[0], streams, axis=0), "section")
-        fields = turn(fields, "section")
+        own_fields = lax.dynamic_index_in_dim(fields, section_place, 0, keepdims=False)
+        first_routes = [own_fields]
+        later_routes = [own_fields]
+        for r in range(1, sections):
+            target = (section_place + r) % sections
+            going = lax.dynamic_index_in_dim(fields, target, 0, keepdims=False)
+            first_routes.append(lax.ppermute(going, "section", [(0, r)]))
+            pairs = [(p, (p + r) % sections) for p in range(1, sections)]
+            later_routes.append(lax.ppermute(going, "section", pairs))
         owner_index = channel // local_channels
         owner_hot = (owner_index[:, :, None] == jnp.arange(owners)).astype(jnp.int32)
         ranking = jnp.sum((jnp.cumsum(owner_hot, axis=1) - 1) * owner_hot, axis=2)
@@ -135,7 +173,11 @@
             sent = select_rows(asked_hot[w], beta, ((1,), (1,)))
             got = turn(sent.reshape(owners, capacity, pred_count), "obs")
             block_coeffs = select_rows(got.reshape(slots, pred_count), placing[w], ((0,), (1,)))
-            block_sums, statistics = block_rows(fields[w], block_coeffs, pred_count)
+            if w == 1:
+                later_routes, block_coeffs = lax.optimization_barrier((later_routes, block_coeffs))
+            routes = first_routes if w == 0 else later_routes
+            window_fields = lax.select_n((section_place - w) % sections, *routes)
+            block_sums, statistics = block_rows(window_fields, block_coeffs, pred_count)
             rows = select_rows(placing[w], block_sums, ((0,), (0,)))
             rows = jnp.concatenate(
                 [rows, jnp.broadcast_to(statistics[None], (slots, 2))], axis=1
@@ -143,18 +185,15 @@
             rows = turn(rows, "obs")
             totals = jnp.sum(rows[:, 0, column_count:], axis=0)
             inflation = (totals[0] + PRIOR_WEIGHT) / (totals[1] + PRIOR_WEIGHT)
-            normal = (
-                select_rows(
-                    rows.reshape(slots, column_count + 2)[:, :column_count],
-                    asked_hot[w],
-                    ((0,), (0,)),
-                )
-                / inflation
+            normal = select_rows(
+                rows.reshape(slots, column_count + 2)[:, :column_count],
+                asked_hot[w],
+                ((0,), (0,)),
             )
-            info_post = kept_info + normal[:tri_count]
-            beta = beta + solve_packed(info_post, normal[tri_count:])
-            kept_info = memory_factor[None] * info_post
-            results.append(jnp.concatenate([beta, info_post], axis=0))
+            result = update_state(normal, kept_info, beta, inflation)
+            beta = result[:pred_count]
+            kept_info = memory_factor[None] * result[pred_count:]
+            results.append(result)
         landed = turn(jnp.stack(results), "section")
         count = min(sections, stream_count - group * sections)
         coeff_parts.append(landed[:count, :pred_count])

time: 213 us -> 201 us (0.944)
  blocking collectives: 61 us -> 35.1 us
  starting transfers between devices: 24.2 us -> 42.9 us
  other arithmetic: 36.2 us -> 23.5 us
  Pallas kernels: 0 us -> 10.3 us
  local copies, waits for them, and re-layouts: 31.9 us -> 25.1 us
  waiting for transfers between devices: 38.9 us -> 44.2 us
    all_to_all x6 -> x3, blocking collectives: 61 us -> 35.1 us  [turn(): return lax.all_to_all(array, axis, split_axis=0, concat_axis=0, tiled=True)]
    div x32 -> x0, other arithmetic: 18 us -> none  [the longest x8 7.68 us: solve_packed(): (target[i] - sum((factor[i][k] * forward[k] for k in range(i)))) / factor...]
    ppermute x0 -> x6, starting transfers between devices: none -> 13.6 us  [the longest x3 9.7 us: local(): first_routes.append(lax.ppermute(going, 'section', [(0, r)]))]
    pallas_call x0 -> x4, Pallas kernels: none -> 10.3 us  [update_state(): pl.pallas_call(update_kernel, out_shape=jax.ShapeDtypeStruct(normal.shape...]
    another operation x8 -> x1, local copies, waits for them, and re-layouts: 6.79 us -> 0.01 us  [the longest x7 6.79 us: solve_packed(): return jnp.stack(backward)]
    all_to_all x6 -> x8, waiting for transfers between devices: 38.9 us -> 44.2 us  [turn(): return lax.all_to_all(array, axis, split_axis=0, concat_axis=0, tiled=True)]
    all_to_all x6 -> x8, starting transfers between devices: 24.2 us -> 29.3 us  [turn(): return lax.all_to_all(array, axis, split_axis=0, concat_axis=0, tiled=True)]
    mul x8 -> x4, local copies, waits for them, and re-layouts: 4.22 us -> 0.58 us  [block_rows(): offset = jnp.sum(shaped * block_coeffs[:, :, None], axis=0)]
  transfers between devices with their start and end apart: 6 -> 14, of which waited for: 5 -> 8; matrix products, arithmetic and copies ran while one was open for 6% -> 11% of each run, Pallas kernels for 0% -> 1%
where the time goes in v2:
time: 201 us; the launch traced here: 200 us
  waiting for transfers between devices  44.2 us (22%)
  starting transfers between devices  42.9 us (21%)
  blocking collectives  35.1 us (17%)
  local copies, waits for them, and re-layouts  25.1 us (12%)
  other arithmetic  23.5 us (12%)
  Pallas kernels  10.3 us (5%)
  matrix products  9.67 us (5%)
  between operations  8.88 us (4%)
    all_to_all x8, waiting for transfers between devices, turn(): return lax.all_to_all(array, axis, split_axis=0, concat_axis=0, tiled=True)  44.2 us
    all_to_all x3, blocking collectives, turn(): return lax.all_to_all(array, axis, split_axis=0, concat_axis=0, tiled=True)  35.1 us
    all_to_all x8, starting transfers between devices, turn(): return lax.all_to_all(array, axis, split_axis=0, concat_axis=0, tiled=True)  29.3 us
    pallas_call x4, Pallas kernels, update_state(): pl.pallas_call(update_kernel, out_shape=jax.ShapeDtypeStruct(normal.shape...  10.3 us
    ppermute x3, starting transfers between devices, local(): first_routes.append(lax.ppermute(going, 'section', [(0, r)]))  9.7 us
    dot_general x16, matrix products, select_rows(): lax.dot_general(hot, values, (dims, ((), ())), precision=highest, preferr...  8.7 us
    unnamed x47, local copies, waits for them, and re-layouts  7.98 us
    another operation x4, other arithmetic, block_rows(): jnp.stack([chi_square, passed_count])  5.42 us
  transfers between devices with their start and end apart: 14, of which 8 were waited for; matrix products, arithmetic and copies ran while one was open for 11% of the time, Pallas kernels for 1%

profile of v2, /device:TPU:0, one launch (start us, length us, event | category | flops | bytes accessed | tf_op | source)
XLA Modules:
  0.0 199.6 jit_solution(13625406565641800431)
XLA Ops:
  11.6 3.8 %collective-permute-start.1 = (f32[22,4096]{1,0:T(8,128)S(1)}, f32[22,4096]{1,0:T(8,128)S(1)}, u32[]{:S(2)}, u32[]{:S(2)}) collective-permute-start(f32[22,4096]{1,0:T(8,128)S(1)} %get-tuple-element.56), channel_id=1, source_target_pairs={{0,16},{1,17},{2,18},{3,19},{4,20},{5,21},{6,22},{7,23}} | collective-permute-start | bytes 1081352 | tf_op jit(solution)/shard_map/ppermute | solution.py:155
  16.7 3.5 %collective-permute-start.2 = (f32[22,4096]{1,0:T(8,128)S(1)}, f32[22,4096]{1,0:T(8,128)}, u32[]{:S(2)}, u32[]{:S(2)}) collective-permute-start(f32[22,4096]{1,0:T(8,128)S(1)} %get-tuple-element.55), channel_id=1, source_target_pairs={{0,24},{1,25},{2,26},{3,27},{4,28},{5,29},{6,30},{7,31}} | collective-permute-start | bytes 1081352 | tf_op jit(solution)/shard_map/ppermute | solution.py:155
  21.4 3.2 %all-to-all-start = ((s32[4,1,32]{2,1,0:T(1,128)}), s32[4,1,32]{2,1,0:T(1,128)S(1)}, u32[]{:S(2)}, u32[]{:S(2)}) async-start(s32[4,1,32]{2,1,0:T(1,128)} %bitcast.4), calls=%async_computation | async-start | bytes 4096 | tf_op jit(solution)/shard_map/all_to_all | solution.py:126
  28.1 3.0 %all-to-all-done = s32[4,1,32]{2,1,0:T(1,128)S(1)} async-done(((s32[4,1,32]{2,1,0:T(1,128)}), s32[4,1,32]{2,1,0:T(1,128)S(1)}, u32[]{:S(2)}, u32[]{:S(2)}) %all-to-all-start) | async-done | bytes 544 | tf_op jit(solution)/shard_map/all_to_all | solution.py:126
  32.3 5.8 %all-to-all-start.1 = ((s32[8,4,8]{2,1,0:T(4,128)}), s32[8,4,8]{2,1,0:T(4,128)S(1)}, u32[]{:S(2)}, u32[]{:S(2)}) async-start(s32[8,4,8]{2,1,0:T(4,128)} %copy.120), calls=%async_computation.1 | async-start | bytes 32768 | tf_op jit(solution)/shard_map/all_to_all | solution.py:126
  38.7 5.9 %all-to-all-done.1 = s32[8,4,8]{2,1,0:T(4,128)S(1)} async-done(((s32[8,4,8]{2,1,0:T(4,128)}), s32[8,4,8]{2,1,0:T(4,128)S(1)}, u32[]{:S(2)}, u32[]{:S(2)}) %all-to-all-start.1) | async-done | bytes 1056 | tf_op jit(solution)/shard_map/all_to_all | solution.py:126
  45.7 3.3 %all-to-all-start.2 = ((f32[8,1,160]{2,1,0:T(1,128)}), f32[8,1,160]{2,1,0:T(1,128)S(1)}, u32[]{:S(2)}, u32[]{:S(2)}) async-start(f32[8,1,160]{2,1,0:T(1,128)} %reshape.482), calls=%async_computation.2 | async-start | bytes 16384 | tf_op jit(solution)/shard_map/all_to_all | solution.py:126
  49.2 6.4 %all-to-all-done.2 = f32[8,1,160]{2,1,0:T(1,128)S(1)} async-done(((f32[8,1,160]{2,1,0:T(1,128)}), f32[8,1,160]{2,1,0:T(1,128)S(1)}, u32[]{:S(2)}, u32[]{:S(2)}) %all-to-all-start.2) | async-done | bytes 5152 | tf_op jit(solution)/shard_map/all_to_all | solution.py:126
  64.7 3.4 %all-to-all-start.3 = ((f32[8,8,232]{2,1,0:T(8,128)}), f32[8,8,232]{2,1,0:T(8,128)S(1)}, u32[]{:S(2)}, u32[]{:S(2)}) async-start(f32[8,8,232]{2,1,0:T(8,128)} %maximum_bitcast_fusion), calls=%async_computation.3 | async-start | bytes 131072 | tf_op jit(solution)/shard_map/all_to_all | solution.py:126
  69.0 6.2 %all-to-all-done.3 = f32[8,8,232]{2,1,0:T(8,128)S(1)} async-done(((f32[8,8,232]{2,1,0:T(8,128)}), f32[8,8,232]{2,1,0:T(8,128)S(1)}, u32[]{:S(2)}, u32[]{:S(2)}) %all-to-all-start.3) | async-done | bytes 59424 | tf_op jit(solution)/shard_map/all_to_all | solution.py:126
  78.1 2.6 %update_state.4 = f32[230,256]{1,0:T(8,128)} custom-call(f32[230,256]{1,0:T(8,128)} %fusion.18.normal_ref, f32[210,256]{1,0:T(8,128)} %bitcast.211, f32[20,256]{1,0:T(8,128)} %bitcast.225, f32[1,1]{1,0:T(1,128)} %bitcast.33.inflation_ref), custom_call_target="tpu_custom_call" | custom-call | tf_op jit(solution)/shard_map/update_state/pallas_call | solution.py:65
  82.3 3.3 %all-to-all-start.4 = ((f32[8,1,160]{2,1,0:T(1,128)}), f32[8,1,160]{2,1,0:T(1,128)S(1)}, u32[]{:S(2)}, u32[]{:S(2)}) async-start(f32[8,1,160]{2,1,0:T(1,128)} %reshape.484), calls=%async_computation.4 | async-start | bytes 16384 | tf_op jit(solution)/shard_map/all_to_all | solution.py:126
  85.7 6.4 %all-to-all-done.4 = f32[8,1,160]{2,1,0:T(1,128)S(1)} async-done(((f32[8,1,160]{2,1,0:T(1,128)}), f32[8,1,160]{2,1,0:T(1,128)S(1)}, u32[]{:S(2)}, u32[]{:S(2)}) %all-to-all-start.4) | async-done | bytes 5152 | tf_op jit(solution)/shard_map/all_to_all | solution.py:126
  99.7 3.4 %all-to-all-start.5 = ((f32[8,8,232]{2,1,0:T(8,128)}), f32[8,8,232]{2,1,0:T(8,128)S(1)}, u32[]{:S(2)}, u32[]{:S(2)}) async-start(f32[8,8,232]{2,1,0:T(8,128)} %maximum_bitcast_fusion.1), calls=%async_computation.5 | async-start | bytes 131072 | tf_op jit(solution)/shard_map/all_to_all | solution.py:126
  104.4 5.5 %all-to-all-done.5 = f32[8,8,232]{2,1,0:T(8,128)S(1)} async-done(((f32[8,8,232]{2,1,0:T(8,128)}), f32[8,8,232]{2,1,0:T(8,128)S(1)}, u32[]{:S(2)}, u32[]{:S(2)}) %all-to-all-start.5) | async-done | bytes 59424 | tf_op jit(solution)/shard_map/all_to_all | solution.py:126
  112.9 2.6 %update_state.5 = f32[230,256]{1,0:T(8,128)} custom-call(f32[230,256]{1,0:T(8,128)} %fusion.16.normal_ref, f32[210,256]{1,0:T(8,128)} %slice_multiply_fusion.2.kept_ref, f32[20,256]{1,0:T(8,128)} %slice.211.beta_ref, f32[1,1]{1,0:T(1,128)} %bitcast.50.inflation_ref), custom_call_target="tpu_custom_call" | custom-call | tf_op jit(solution)/shard_map/update_state/pallas_call | solution.py:65
  116.5 8.9 %all_to_all.59 = f32[8,1,160]{2,1,0:T(1,128)S(1)} all-to-all(f32[8,1,160]{2,1,0:T(1,128)S(1)} %reshape.486), channel_id=1, replica_groups=mesh['section'=4,'obs'=8] {'obs'}, dimensions={0} | all-to-all | bytes 10240 | tf_op jit(solution)/shard_map/all_to_all | solution.py:126
  131.6 3.5 %all-to-all-start.7 = ((f32[8,8,232]{2,1,0:T(8,128)}), f32[8,8,232]{2,1,0:T(8,128)S(1)}, u32[]{:S(2)}, u32[]{:S(2)}) async-start(f32[8,8,232]{2,1,0:T(8,128)} %maximum_bitcast_fusion.2), calls=%async_computation.7 | async-start | bytes 131072 | tf_op jit(solution)/shard_map/all_to_all | solution.py:126
  136.4 5.3 %all-to-all-done.7 = f32[8,8,232]{2,1,0:T(8,128)S(1)} async-done(((f32[8,8,232]{2,1,0:T(8,128)}), f32[8,8,232]{2,1,0:T(8,128)S(1)}, u32[]{:S(2)}, u32[]{:S(2)}) %all-to-all-start.7) | async-done | bytes 59424 | tf_op jit(solution)/shard_map/all_to_all | solution.py:126
  144.8 2.6 %update_state.6 = f32[230,256]{1,0:T(8,128)} custom-call(f32[230,256]{1,0:T(8,128)} %fusion.14.normal_ref, f32[210,256]{1,0:T(8,128)} %slice_multiply_fusion.1.kept_ref, f32[20,256]{1,0:T(8,128)} %slice.223.beta_ref, f32[1,1]{1,0:T(1,128)} %bitcast.67.inflation_ref), custom_call_target="tpu_custom_call" | custom-call | tf_op jit(solution)/shard_map/update_state/pallas_call | solution.py:65
  148.4 8.9 %all_to_all.60 = f32[8,1,160]{2,1,0:T(1,128)S(1)} all-to-all(f32[8,1,160]{2,1,0:T(1,128)S(1)} %reshape.488), channel_id=1, replica_groups=mesh['section'=4,'obs'=8] {'obs'}, dimensions={0} | all-to-all | bytes 10240 | tf_op jit(solution)/shard_map/all_to_all | solution.py:126
  163.5 3.4 %all-to-all-start.9 = ((f32[8,8,232]{2,1,0:T(8,128)}), f32[8,8,232]{2,1,0:T(8,128)S(1)}, u32[]{:S(2)}, u32[]{:S(2)}) async-start(f32[8,8,232]{2,1,0:T(8,128)} %maximum_bitcast_fusion.3), calls=%async_computation.9 | async-start | bytes 131072 | tf_op jit(solution)/shard_map/all_to_all | solution.py:126
  168.2 5.5 %all-to-all-done.9 = f32[8,8,232]{2,1,0:T(8,128)S(1)} async-done(((f32[8,8,232]{2,1,0:T(8,128)}), f32[8,8,232]{2,1,0:T(8,128)S(1)}, u32[]{:S(2)}, u32[]{:S(2)}) %all-to-all-start.9) | async-done | bytes 59424 | tf_op jit(solution)/shard_map/all_to_all | solution.py:126
  180.3 17.3 %all_to_all.61 = f32[4,230,256]{2,1,0:T(8,128)S(1)} all-to-all(f32[4,230,256]{2,1,0:T(8,128)S(1)} %pad_maximum_fusion.1), channel_id=1, replica_groups=mesh['section'=4,'obs'=8] {'section'}, dimensions={0} | all-to-all | bytes 1884160 | tf_op jit(solution)/shard_map/all_to_all | solution.py:126
  (191 shorter events, 67.1 us)
Async XLA Ops:
  0.6 67.4 %copy-start = (f32[4,210,256]{2,0,1:T(4,128)S(1)}, f32[4,210,256]{2,0,1:T(4,128)}, u32[]{:S(2)}) copy-start(f32[4,210,256]{2,0,1:T(4,128)} %param.28) | copy-start | bytes 2580484
  0.6 3.0 %copy-start.3 = (f32[1,4,4096]{2,1,0:T(4,128)S(1)}, f32[1,4,4096]{2,1,0:T(4,128)}, u32[]{:S(2)}) copy-start(f32[1,4,4096]{2,1,0:T(4,128)} %param.22) | copy-start | bytes 196612
  0.7 3.8 %copy-start.7 = (bf16[1,4,20,4096]{3,1,2,0:T(4,128)(2,1)S(1)}, bf16[1,4,20,4096]{3,1,2,0:T(4,128)(2,1)}, u32[]{:S(2)}) copy-start(bf16[1,4,20,4096]{3,1,2,0:T(4,128)(2,1)} %param.21) | copy-start | bytes 1966084
  7.0 13.2 %copy-start.8 = (s32[1,4,32]{2,1,0:T(4,128)S(1)}, s32[1,4,32]{2,1,0:T(4,128)}, u32[]{:S(2)}) copy-start(s32[1,4,32]{2,1,0:T(4,128)} %param.25) | copy-start | bytes 1540
  7.0 17.6 %copy-start.1 = (s32[4]{0:T(128)S(1)}, s32[4]{0:T(128)}, u32[]{:S(2)}) copy-start(s32[4]{0:T(128)} %param.26) | copy-start | bytes 52
  7.0 31.1 %copy-start.10 = (s32[210]{0:T(256)S(1)}, s32[210]{0:T(256)}, u32[]{:S(2)}) copy-start(s32[210]{0:T(256)} %constant.183) | copy-start | bytes 2524
  7.9 49.7 %collective-permute-start = (f32[22,4096]{1,0:T(8,128)}, f32[22,4096]{1,0:T(8,128)S(1)}, u32[]{:S(2)}, u32[]{:S(2)}) collective-permute-start(f32[22,4096]{1,0:T(8,128)} %get-tuple-element.54), channel_id=1, source_target_pairs={{0,8},{1,9},{2,10},{3,11},{4,12},{5,13},{6,14},{7,15}} | collective-permute-start | bytes 1081352 | tf_op jit(solution)/shard_map/ppermute | solution.py:155
  10.3 82.8 %collective-permute-start.3 = (f32[22,4096]{1,0:T(8,128)}, f32[22,4096]{1,0:T(8,128)S(1)}, u32[]{:S(2)}, u32[]{:S(2)}) collective-permute-start(f32[22,4096]{1,0:T(8,128)} %get-tuple-element.54), channel_id=1, source_target_pairs={{8,16},{16,24},{24,0},{9,17},{17,25},{25,1},{10,18},{18,26},{26,2}... | collective-permute-start | bytes 1081352 | tf_op jit(solution)/shard_map/ppermute | solution.py:157
  11.6 47.3 %collective-permute-start.1 = (f32[22,4096]{1,0:T(8,128)S(1)}, f32[22,4096]{1,0:T(8,128)S(1)}, u32[]{:S(2)}, u32[]{:S(2)}) collective-permute-start(f32[22,4096]{1,0:T(8,128)S(1)} %get-tuple-element.56), channel_id=1, source_target_pairs={{0,16},{1,17},{2,18},{3,19},{4,20},{5,21},{6,22},{7,23}} | collective-permute-start | bytes 1081352 | tf_op jit(solution)/shard_map/ppermute | solution.py:155
  15.4 77.8 %collective-permute-start.4 = (f32[22,4096]{1,0:T(8,128)S(1)}, f32[22,4096]{1,0:T(8,128)}, u32[]{:S(2)}, u32[]{:S(2)}) collective-permute-start(f32[22,4096]{1,0:T(8,128)S(1)} %get-tuple-element.56), channel_id=1, source_target_pairs={{8,24},{16,0},{24,8},{9,25},{17,1},{25,9},{10,26},{18,2},{26,10},{... | collective-permute-start | bytes 1081352 | tf_op jit(solution)/shard_map/ppermute | solution.py:157
  16.7 42.2 %collective-permute-start.2 = (f32[22,4096]{1,0:T(8,128)S(1)}, f32[22,4096]{1,0:T(8,128)}, u32[]{:S(2)}, u32[]{:S(2)}) collective-permute-start(f32[22,4096]{1,0:T(8,128)S(1)} %get-tuple-element.55), channel_id=1, source_target_pairs={{0,24},{1,25},{2,26},{3,27},{4,28},{5,29},{6,30},{7,31}} | collective-permute-start | bytes 1081352 | tf_op jit(solution)/shard_map/ppermute | solution.py:155
  21.4 9.6 %all-to-all-start = ((s32[4,1,32]{2,1,0:T(1,128)}), s32[4,1,32]{2,1,0:T(1,128)S(1)}, u32[]{:S(2)}, u32[]{:S(2)}) async-start(s32[4,1,32]{2,1,0:T(1,128)} %bitcast.4), calls=%async_computation | async-start | bytes 4096 | tf_op jit(solution)/shard_map/all_to_all | solution.py:126
  32.3 12.4 %all-to-all-start.1 = ((s32[8,4,8]{2,1,0:T(4,128)}), s32[8,4,8]{2,1,0:T(4,128)S(1)}, u32[]{:S(2)}, u32[]{:S(2)}) async-start(s32[8,4,8]{2,1,0:T(4,128)} %copy.120), calls=%async_computation.1 | async-start | bytes 32768 | tf_op jit(solution)/shard_map/all_to_all | solution.py:126
  45.7 9.8 %all-to-all-start.2 = ((f32[8,1,160]{2,1,0:T(1,128)}), f32[8,1,160]{2,1,0:T(1,128)S(1)}, u32[]{:S(2)}, u32[]{:S(2)}) async-start(f32[8,1,160]{2,1,0:T(1,128)} %reshape.482), calls=%async_computation.2 | async-start | bytes 16384 | tf_op jit(solution)/shard_map/all_to_all | solution.py:126
  57.6 35.6 %collective-permute-start.5 = (f32[22,4096]{1,0:T(8,128)S(1)}, f32[22,4096]{1,0:T(8,128)}, u32[]{:S(2)}, u32[]{:S(2)}) collective-permute-start(f32[22,4096]{1,0:T(8,128)S(1)} %get-tuple-element.55), channel_id=1, source_target_pairs={{8,0},{16,8},{24,16},{9,1},{17,9},{25,17},{10,2},{18,10},{26,18},{... | collective-permute-start | bytes 1081352 | tf_op jit(solution)/shard_map/ppermute | solution.py:157
  64.7 10.5 %all-to-all-start.3 = ((f32[8,8,232]{2,1,0:T(8,128)}), f32[8,8,232]{2,1,0:T(8,128)S(1)}, u32[]{:S(2)}, u32[]{:S(2)}) async-start(f32[8,8,232]{2,1,0:T(8,128)} %maximum_bitcast_fusion), calls=%async_computation.3 | async-start | bytes 131072 | tf_op jit(solution)/shard_map/all_to_all | solution.py:126
  82.3 9.8 %all-to-all-start.4 = ((f32[8,1,160]{2,1,0:T(1,128)}), f32[8,1,160]{2,1,0:T(1,128)S(1)}, u32[]{:S(2)}, u32[]{:S(2)}) async-start(f32[8,1,160]{2,1,0:T(1,128)} %reshape.484), calls=%async_computation.4 | async-start | bytes 16384 | tf_op jit(solution)/shard_map/all_to_all | solution.py:126
  95.8 7.2 %copy-start.4 = (f32[230,256]{1,0:T(8,128)S(1)}, f32[230,256]{1,0:T(8,128)}, u32[]{:S(2)}) copy-start(f32[230,256]{1,0:T(8,128)} %update_state.4) | copy-start | bytes 706564
  95.8 7.2 %copy-start.9 = (f32[256]{0:T(256)S(1)}, f32[256]{0:T(256)}, u32[]{:S(2)}) copy-start(f32[256]{0:T(256)} %param.29) | copy-start | bytes 3076
  99.7 10.2 %all-to-all-start.5 = ((f32[8,8,232]{2,1,0:T(8,128)}), f32[8,8,232]{2,1,0:T(8,128)S(1)}, u32[]{:S(2)}, u32[]{:S(2)}) async-start(f32[8,8,232]{2,1,0:T(8,128)} %maximum_bitcast_fusion.1), calls=%async_computation.5 | async-start | bytes 131072 | tf_op jit(solution)/shard_map/all_to_all | solution.py:126
  127.7 7.4 %copy-start.5 = (f32[230,256]{1,0:T(8,128)S(1)}, f32[230,256]{1,0:T(8,128)}, u32[]{:S(2)}) copy-start(f32[230,256]{1,0:T(8,128)} %update_state.5) | copy-start | bytes 706564
  131.6 10.2 %all-to-all-start.7 = ((f32[8,8,232]{2,1,0:T(8,128)}), f32[8,8,232]{2,1,0:T(8,128)S(1)}, u32[]{:S(2)}, u32[]{:S(2)}) async-start(f32[8,8,232]{2,1,0:T(8,128)} %maximum_bitcast_fusion.2), calls=%async_computation.7 | async-start | bytes 131072 | tf_op jit(solution)/shard_map/all_to_all | solution.py:126
  159.6 7.2 %copy-start.6 = (f32[230,256]{1,0:T(8,128)S(1)}, f32[230,256]{1,0:T(8,128)}, u32[]{:S(2)}) copy-start(f32[230,256]{1,0:T(8,128)} %update_state.6) | copy-start | bytes 706564
  163.5 10.2 %all-to-all-start.9 = ((f32[8,8,232]{2,1,0:T(8,128)}), f32[8,8,232]{2,1,0:T(8,128)S(1)}, u32[]{:S(2)}, u32[]{:S(2)}) async-start(f32[8,8,232]{2,1,0:T(8,128)} %maximum_bitcast_fusion.3), calls=%async_computation.9 | async-start | bytes 131072 | tf_op jit(solution)/shard_map/all_to_all | solution.py:126
  (1 other events, 1.2 us)
